TPU v7x, 32 devices: a whole 2x2x4 slice. The times are simulated.
32 devices in a mesh: data: 2 (over x), seq: 4 (over z), dap: 4 (over y, core).
Axes of the slice: x: 2, y: 2, z: 4, core: 2. Of those that a mesh axis runs over, the one named last changes fastest.
Arguments:
- msa_act: bfloat16 [1024, 512, 64], P(('data', 'seq', 'dap')), parts along dimension 0
- msa_mask: int32 [1024, 512], P(('data', 'seq', 'dap')), parts along dimension 0
- pair_act: float32 [1024, 512, 128], P(('data', 'dap')), parts along dimension 0
- ln_gamma: bfloat16 [64], replicated
- ln_beta: bfloat16 [64], replicated
- w_a: bfloat16 [64, 32], replicated
- b_a: bfloat16 [32], replicated
- w_b: bfloat16 [64, 32], replicated
- b_b: bfloat16 [32], replicated
- w_out: bfloat16 [1024, 128], replicated
- b_out: bfloat16 [128], replicated
Outputs:
- output: float32 [1024, 512, 128], P(('data', 'dap')), parts along dimension 0
There are 2 independent parts. A program takes and returns all parts, laid end to end along the dimension named above; an argument that names none is the same for every part.
All inputs are finite; a program needn't handle non-finite values.
Results may differ from a plain program's by a relative error of at most 0.0123679.
Values are sent between devices in bfloat16 or wider.
A program may use at most 1 GiB of HBM per device.

v0:
```python
import jax
import jax.numpy as jnp
from jax import lax
from jax.sharding import PartitionSpec as P


def layer_norm(value_a7, ln_gamma, ln_beta):
    values = value_a7.astype(jnp.float32)
    row_mean = jnp.mean(values, axis=-1, keepdims=True)
    centered = values - row_mean
    variance = jnp.mean(centered * centered, axis=-1, keepdims=True)
    normed = centered * lax.rsqrt(variance + 1e-5)
    return (normed * ln_gamma.astype(jnp.float32) + ln_beta.astype(jnp.float32)).astype(jnp.bfloat16)


def project(normed, weight, bias_vec, seq_keep):
    summed = jnp.einsum('...k,kc->...c', normed, weight, preferred_element_type=jnp.float32)
    return ((summed + bias_vec.astype(jnp.float32)) * seq_keep[..., None]).astype(jnp.bfloat16)


def solution(mesh):
    value_a8 = P(('data', 'seq', 'dap'), None, None)
    mask_spec = P(('data', 'seq', 'dap'), None)
    pair_spec = P(('data', 'dap'), None, None)

    def device_step(value_a9, mask_local, pair_local, ln_gamma, ln_beta, w_a, b_a, w_b, b_b, w_out, b_out):
        hidden = w_a.shape[1]
        pair_dim = w_out.shape[1]
        normed = layer_norm(value_a9, ln_gamma, ln_beta)
        seq_keep = mask_local.astype(jnp.bfloat16)
        left = project(normed, w_a, b_a, seq_keep)
        right = project(normed, w_b, b_b, seq_keep)
        w_cube = w_out.reshape(hidden, hidden, pair_dim)
        lifted = jnp.einsum('sic,cde->side', left, w_cube, preferred_element_type=jnp.float32).astype(jnp.bfloat16)
        part_r = jnp.einsum('side,sjd->ije', lifted, right, preferred_element_type=jnp.float32).astype(jnp.bfloat16)
        part_n = jnp.einsum('si,sj->ij', seq_keep, seq_keep, preferred_element_type=jnp.float32)
        rows_r = lax.psum_scatter(part_r, 'dap', scatter_dimension=0, tiled=True)
        rows_n = lax.psum_scatter(part_n, 'dap', scatter_dimension=0, tiled=True)
        rows_r = lax.psum(rows_r, 'seq')
        rows_n = lax.psum(rows_n, 'seq')
        update = (rows_r.astype(jnp.float32) + b_out.astype(jnp.float32)) / (1e-3 + rows_n[..., None])
        return pair_local + update

    return jax.shard_map(device_step, mesh=mesh, in_specs=(value_a8, mask_spec, pair_spec, P(), P(), P(), P(), P(), P(), P(), P()), out_specs=pair_spec, check_vma=False)
```

profile of v0, /device:TPU:0, one launch (start us, length us, event | category | flops | bytes accessed | tf_op | source)
XLA Modules:
  0.0 1222.7 jit_solution(15315697834791966459)
XLA Ops:
  6.5 0.0 reduce-scatter.5.cloned.1.call-start
  6.6 2.3 fusion.24
  8.9 0.0 reduce-scatter.7.cloned.1.call-start
  9.0 0.8 convert_convert_fusion
  9.8 2.0 convert_reduce_fusion
  11.9 0.8 fusion.9
  12.7 1.0 fusion.12
  13.7 1.3 copy-done.3
  15.1 0.4 fusion.26
  15.5 1.3 fusion.19
  16.8 6.8 copy.14
  23.7 0.4 fusion.28
  24.1 1.3 fusion.45
  25.4 114.1 %fusion.2 = bf16[512,512,128]{2,1,0:T(8,128)(2,1)} fusion(bf16[32,512,32,1]{2,0,3,1:T(8,128)(2,1)} %copy.14, bf16[32,32,128,1]{2,1,0,3:T(8,128)(2,1)S(1)} %bitcast.37, bf16[32,512,32,1]{1,0,2,3:T(8,128)(2,1)S(1)} %fusion.45), kind=kOutput, calls=%fused_computation.3 | convolution fusion | flops 73115107328 | bytes 69468160 | tf_op jit(solution)/shard_map/side,sjd->ije/dot_general | solution.py:35
  139.5 0.0 all-reduce.6.cloned.1.call-start
  139.6 0.0 reduce-scatter.5.cloned.1.call-done
  139.6 0.7 all-reduce.6.cloned.1.call-update
  140.3 0.0 all-reduce.4.cloned.1.call-start
  140.3 448.3 %reduce-scatter.7.cloned.1.call-done = bf16[128,512,128]{2,1,0:T(8,128)(2,1)} async-done(((bf16[512,512,128]{2,1,0:T(8,128)(2,1)}), bf16[128,512,128]{2,1,0:T(8,128)(2,1)}) %reduce-scatter.7.cloned.1.call-update) | async-done | bytes 16777232
  588.6 0.6 copy-done.11
  589.2 37.2 %all-reduce.6.cloned.1.call-done = f32[128,512]{1,0:T(8,128)} async-done(((f32[128,512]{1,0:T(8,128)}), f32[128,512]{1,0:T(8,128)}) %all-reduce.6.cloned.1.call-update) | async-done | bytes 262160 | tf_op jit(solution)/shard_map/psum | solution.py:40
  626.4 1.0 broadcast_add_fusion
  627.4 560.7 %all-reduce.4.cloned.1.call-done = bf16[128,512,128]{2,1,0:T(8,128)(2,1)} async-done(((bf16[128,512,128]{2,1,0:T(8,128)(2,1)}), bf16[128,512,128]{2,1,0:T(8,128)(2,1)}) %all-reduce.4.cloned.1.call-update) | async-done | bytes 16777232 | tf_op jit(solution)/shard_map/psum | solution.py:39
  1188.1 28.1 %divide_add_fusion = f32[128,512,128]{2,1,0:T(8,128)} fusion(f32[128,512,128]{2,1,0:T(8,128)} %param.13, bf16[128,512,128]{2,1,0:T(8,128)(2,1)} %all-reduce.4.cloned.1.call-done, f32[128,512]{1,0:T(8,128)S(1)} %broadcast_add_fusion, f32[128]{0:T(128)S(1)} %convert_element_type.61), kind=kLoop, calls=%fused_computation.5 | loop fusion | flops 33554432 | bytes 84148736 | tf_op jit(solution)/shard_map/add | solution.py:42
  (32 shorter events, 0.1 us)
Async XLA Ops:
  6.5 18.9 %copy-start = (bf16[1024,128]{1,0:T(8,128)(2,1)S(1)}, bf16[1024,128]{1,0:T(8,128)(2,1)}, u32[]{:S(2)}) copy-start(bf16[1024,128]{1,0:T(8,128)(2,1)} %param.20) | copy-start | bytes 786436
  6.5 5.3 copy-start.2
  6.5 6.1 copy-start.7
  6.5 6.2 copy-start.8
  6.5 6.2 copy-start.9
  6.5 133.0 %reduce-scatter.5.cloned.1.call-start = ((), (), s32[]{:S(2)}) async-start(), calls=%async_computation.3 | async-start | bytes 1310720 | tf_op jit(solution)/shard_map/reduce_scatter | solution.py:38
  8.9 579.6 %reduce-scatter.7.cloned.1.call-start = ((), (), s32[]{:S(2)}) async-start(), calls=%async_computation.5 | async-start | bytes 83886080
  9.8 5.2 copy-start.5
  13.7 1.4 copy-start.3
  15.5 8.2 copy-start.4
  15.5 8.2 copy-start.6
  16.8 7.3 copy-start.10
  139.5 486.9 %all-reduce.6.cloned.1.call-start = ((), (), s32[]{:S(2)}) async-start(), calls=%async_computation.4 | async-start | bytes 524288 | tf_op jit(solution)/shard_map/psum | solution.py:40
  140.3 1047.8 %all-reduce.4.cloned.1.call-start = ((), (), s32[]{:S(2)}) async-start(), calls=%async_computation.2 | async-start | bytes 33554432 | tf_op jit(solution)/shard_map/psum | solution.py:39
  588.6 0.7 copy-start.11
  1188.1 28.1 %copy-start.1 = (bf16[1024,128]{1,0:T(8,128)(2,1)S(1)}, bf16[1024,128]{1,0:T(8,128)(2,1)}, u32[]{:S(2)}) copy-start(bf16[1024,128]{1,0:T(8,128)(2,1)} %param.20) | copy-start | bytes 786436
Sparse Core Ops, SparseCore 0:
  9.9 27.4 reduce-scatter.4
  139.6 448.8 reduce-scatter.6
  590.9 35.4 all-reduce.5
  628.7 559.2 all-reduce.3
where the time goes:
time: 1220 us
  waiting for transfers between devices  1050 us (86%)
  matrix products  117 us (10%)
  other arithmetic  36.3 us (3%)
  between operations  13.3 us (1%)
    psum x1, waiting for transfers between devices, device_step(): rows_r = lax.psum(rows_r, 'seq')  561 us
    unnamed x5, waiting for transfers between devices  449 us
    dot_general x1, matrix products, device_step(): jnp.einsum('side,sjd->ije', lifted, right, preferred_element_type=jnp.flo...  114 us
    psum x1, waiting for transfers between devices, device_step(): rows_n = lax.psum(rows_n, 'seq')  37.2 us
    add x1, other arithmetic, device_step(): return pair_local + update  28.1 us
  transfers between devices with their start and end apart: 4, of which 3 were waited for; matrix products, arithmetic and copies ran while one was open for 11% of the time, Pallas kernels for 0%

commit v1 on v0

v1 whole, which is shorter than its diff:
```python
import functools
import jax
import jax.numpy as jnp
from jax import lax
from jax.sharding import PartitionSpec as P
from jax.experimental import pallas as pl
from jax.experimental.pallas import tpu as pltpu

F32 = jnp.float32
BF16 = jnp.bfloat16
VMEM_LIMIT = 60 * 1024 * 1024
S_STEP = 16
I_STEP = 16
J_STEP = 128


def project_kernel(msa_ref, mask_ref, gamma_ref, beta_ref, weight_ref, bias_ref, out_ref, tmp_ref):
    res, width = msa_ref.shape[1:]
    for s in range(S_STEP):
        x = msa_ref[s].astype(F32).T
        mean = jnp.sum(x, axis=0, keepdims=True) * (1.0 / width)
        centered = x - mean
        var = jnp.sum(centered * centered, axis=0, keepdims=True) * (1.0 / width)
        normed = centered * lax.rsqrt(var + 1e-5)
        normed = (normed * gamma_ref[...] + beta_ref[...]).astype(BF16)
        proj = jnp.dot(weight_ref[...], normed, preferred_element_type=F32) + bias_ref[...]
        tmp_ref[s] = proj * mask_ref[s:s + 1, :].astype(F32)
    half = out_ref.shape[1] - 1
    for g in range(2 * half // 8):
        flat = jnp.transpose(tmp_ref[:, g * 8:g * 8 + 8, :], (1, 0, 2)).astype(BF16)
        part, base = divmod(g * 8, half)
        out_ref[part, base:base + 8] = flat
    keep = mask_ref[...].astype(F32).astype(BF16)
    out_ref[0, half] = keep
    out_ref[1, half] = keep


def project(msa, mask, gamma, beta, weight, bias):
    seqs, res, width = msa.shape
    chans = weight.shape[0]
    return pl.pallas_call(
        project_kernel,
        grid=(seqs // S_STEP,),
        in_specs=[
            pl.BlockSpec((S_STEP, res, width), lambda g: (g, 0, 0)),
            pl.BlockSpec((S_STEP, res), lambda g: (g, 0)),
            pl.BlockSpec((width, 1), lambda g: (0, 0)),
            pl.BlockSpec((width, 1), lambda g: (0, 0)),
            pl.BlockSpec((chans, width), lambda g: (0, 0)),
            pl.BlockSpec((chans, 1), lambda g: (0, 0)),
        ],
        out_specs=pl.BlockSpec((2, chans // 2 + 1, S_STEP, res), lambda g: (0, 0, g, 0)),
        out_shape=jax.ShapeDtypeStruct((2, chans // 2 + 1, seqs, res), BF16),
        scratch_shapes=[pltpu.VMEM((S_STEP, chans, res), F32)],
        compiler_params=pltpu.CompilerParams(vmem_limit_bytes=VMEM_LIMIT),
        name='project',
    )(msa, mask, gamma, beta, weight, bias)


def turn_kernel(row_ref, left_ref, out_ref, keep_ref, tmp_ref):
    src, chans, seqs, rows = left_ref.shape
    for c in range(chans):
        block = left_ref[:, c].reshape(src * seqs, rows).astype(F32).T
        if c == chans - 1:
            keep_ref[...] = block.astype(BF16)
        else:
            tmp_ref[c] = block

    @pl.loop(0, rows // 8)
    def _(g):
        start = pl.multiple_of(g * 8, 8)
        block = jnp.transpose(tmp_ref[:, pl.ds(start, 8), :], (1, 0, 2)).astype(BF16)
        out_ref[pl.ds(start, 8)] = block


def turn(row_block, left):
    src, _, chans, seqs, res = left.shape
    rows = res // 4
    total = src * seqs
    return pl.pallas_call(
        turn_kernel,
        grid_spec=pltpu.PrefetchScalarGridSpec(
            num_scalar_prefetch=1,
            grid=(1,),
            in_specs=[pl.BlockSpec((src, None, chans, seqs, rows), lambda g, row: (0, 0, 0, 0, row[0]))],
            out_specs=[
                pl.BlockSpec((rows, chans - 1, total), lambda g, row: (0, 0, 0)),
                pl.BlockSpec((rows, total), lambda g, row: (0, 0)),
            ],
            scratch_shapes=[pltpu.VMEM((chans - 1, rows, total), F32)],
        ),
        out_shape=[
            jax.ShapeDtypeStruct((rows, chans - 1, total), BF16),
            jax.ShapeDtypeStruct((rows, total), BF16),
        ],
        compiler_params=pltpu.CompilerParams(vmem_limit_bytes=VMEM_LIMIT),
        name='turn',
    )(row_block, left)


def product_kernel(left_ref, keep_ref, right_ref, weight_ref, bias_ref, pair_ref, out_ref, outer_ref, scale_ref):
    rows, chans, total = left_ref.shape
    cols = right_ref.shape[-1]
    left = left_ref[...].reshape(rows * chans, total)
    count = jnp.dot(keep_ref[...], right_ref[:, chans].reshape(total, cols), preferred_element_type=F32)
    scale_ref[...] = 1.0 / (1e-3 + count)

    for g in range(chans // 4):
        slab = [right_ref[:, g * 4 + k].reshape(total, cols) for k in range(4)]
        rhs = jnp.concatenate(slab, axis=1)
        for m in range(rows // 8):
            part = left[m * 8 * chans:(m + 1) * 8 * chans]
            prod = jnp.dot(part, rhs, preferred_element_type=F32).astype(BF16)
            for k in range(4):
                at = (g * 4 + k) * chans
                for i in range(8):
                    outer_ref[m * 4 + i // 2, at:at + chans, (i % 2) * cols:(i % 2 + 1) * cols] = (
                        prod[i * chans:(i + 1) * chans, k * cols:(k + 1) * cols])
    for h in range(rows // 2):
        lifted = jnp.dot(weight_ref[...], outer_ref[h], preferred_element_type=F32)
        for k in range(2):
            part = lifted[:, k * cols:(k + 1) * cols] + bias_ref[...]
            part = part * scale_ref[h * 2 + k:h * 2 + k + 1, :]
            out_ref[h * 2 + k] = pair_ref[h * 2 + k] + part.T


def product(left, keep, right, weight, bias, pair):
    rows, chans, total = left.shape
    src, _, _, seqs, res = right.shape
    width = weight.shape[0]
    return pl.pallas_call(
        product_kernel,
        grid=(res // J_STEP, rows // I_STEP),
        in_specs=[
            pl.BlockSpec((I_STEP, chans, total), lambda q, g: (g, 0, 0)),
            pl.BlockSpec((I_STEP, total), lambda q, g: (g, 0)),
            pl.BlockSpec((src, None, chans + 1, seqs, J_STEP), lambda q, g: (0, 1, 0, 0, q)),
            pl.BlockSpec(weight.shape, lambda q, g: (0, 0)),
            pl.BlockSpec(bias.shape, lambda q, g: (0, 0)),
            pl.BlockSpec((I_STEP, J_STEP, width), lambda q, g: (g, q, 0)),
        ],
        out_specs=pl.BlockSpec((I_STEP, J_STEP, width), lambda q, g: (g, q, 0)),
        out_shape=jax.ShapeDtypeStruct(pair.shape, F32),
        scratch_shapes=[pltpu.VMEM((I_STEP // 2, chans * chans, 2 * J_STEP), BF16), pltpu.VMEM((I_STEP, J_STEP), F32)],
        compiler_params=pltpu.CompilerParams(vmem_limit_bytes=VMEM_LIMIT),
        name='product',
    )(left, keep, right, weight, bias, pair)


def solution(mesh):
    msa_spec = P(('data', 'seq', 'dap'), None, None)
    mask_spec = P(('data', 'seq', 'dap'), None)
    pair_spec = P(('data', 'dap'), None, None)

    def device_step(msa, mask, pair, ln_gamma, ln_beta, w_a, b_a, w_b, b_b, w_out, b_out):
        hidden = w_a.shape[1]
        width = w_out.shape[1]
        res = msa.shape[1]
        weight = jnp.concatenate([w_a, w_b], axis=1).T
        bias = jnp.concatenate([b_a, b_b]).astype(F32)[:, None]
        both = project(msa, mask, ln_gamma.astype(F32)[:, None], ln_beta.astype(F32)[:, None], weight, bias)
        lift = w_out.reshape(hidden, hidden, width).transpose(2, 1, 0).reshape(width, hidden * hidden)
        bias_col = jnp.broadcast_to(b_out.astype(F32)[:, None], (width, J_STEP))
        gathered = lax.all_gather(both, ('seq', 'dap'))
        row_block = lax.axis_index('dap').reshape(1).astype(jnp.int32)
        left, keep = turn(row_block, gathered)
        return product(left, keep, gathered, lift, bias_col, pair)

    return jax.shard_map(device_step, mesh=mesh, in_specs=(msa_spec, mask_spec, pair_spec, P(), P(), P(), P(), P(), P(), P(), P()), out_specs=pair_spec, check_vma=False)
```

time: 1220 us -> 317 us (0.26)
  waiting for transfers between devices: 1050 us -> 175 us
  matrix products: 117 us -> 0 us
  Pallas kernels: 0 us -> 117 us
  other arithmetic: 36.3 us -> 2.7 us
    psum x2 -> x0, waiting for transfers between devices: 598 us -> none  [the longest x1 561 us: device_step(): rows_r = lax.psum(rows_r, 'seq')]
    unnamed x5 -> x1, waiting for transfers between devices: 449 us -> 0.02 us
    all_gather x0 -> x1, waiting for transfers between devices: none -> 175 us  [device_step(): gathered = lax.all_gather(both, ('seq', 'dap'))]
    dot_general x4 -> x0, matrix products: 117 us -> none  [the longest x1 114 us: device_step(): jnp.einsum('side,sjd->ije', lifted, right, preferred_element_type=jnp.flo...]
    pallas_call x0 -> x3, Pallas kernels: none -> 117 us  [the longest x1 103 us: product(): pl.pallas_call(product_kernel, grid=(res // J_STEP, rows // I_STEP), in_s...]
    add x2 -> x0, other arithmetic: 29.1 us -> none  [the longest x1 28.1 us: device_step(): return pair_local + update]
  transfers between devices with their start and end apart: 4 -> 1, of which waited for: 3 -> 1; matrix products, arithmetic and copies ran while one was open for 11% -> 0% of each run, Pallas kernels for 0% -> 0%
where the time goes in v1:
time: 317 us; the launch traced here: 316 us
  waiting for transfers between devices  175 us (55%)
  Pallas kernels  117 us (37%)
  between operations  13.4 us (4%)
  local copies, waits for them, and re-layouts  8.51 us (3%)
    all_gather x1, waiting for transfers between devices, device_step(): gathered = lax.all_gather(both, ('seq', 'dap'))  175 us
    pallas_call x1, Pallas kernels, product(): pl.pallas_call(product_kernel, grid=(res // J_STEP, rows // I_STEP), in_s...  103 us
    pallas_call x1, Pallas kernels, turn(): pl.pallas_call(turn_kernel, grid_spec=pltpu.PrefetchScalarGridSpec(num_sc...  7.26 us
    pallas_call x1, Pallas kernels, project(): pl.pallas_call(project_kernel, grid=(seqs // S_STEP,), in_specs=[pl.Block...  6.51 us
  transfers between devices with their start and end apart: 1, of which 1 were waited for; matrix products, arithmetic and copies ran while one was open for 0% of the time, Pallas kernels for 0%

profile of v1, /device:TPU:0, one launch (start us, length us, event | category | flops | bytes accessed | tf_op | source)
XLA Modules:
  0.0 316.2 jit_solution(11671283301344875347)
XLA Ops:
  6.5 0.0 copy-start.1
  6.5 0.0 copy-start.2
  6.5 0.0 all-gather.3.cloned.1.call-start
  6.5 0.7 bitcast_convert_fusion.1
  7.2 0.7 bitcast_convert_fusion
  7.9 0.7 maximum_convert_fusion
  8.6 0.7 copy.40.bias_ref
  9.3 0.7 copy.39.beta_ref
  10.0 0.7 copy.38.gamma_ref
  10.7 4.7 %copy.37.msa_ref = bf16[32,512,64]{2,1,0:T(8,128)(2,1)} copy(bf16[32,512,64]{1,2,0:T(8,128)(2,1)} %param.11) | data formatting | bytes 4194304 | tf_op args[0]
  15.5 0.0 copy-done.1
  15.5 0.0 copy-done.2
  15.5 0.6 maximum_bitcast_fusion.weight_ref
  16.1 0.0 copy-start
  16.1 6.5 %project.1 = bf16[2,33,32,512]{3,2,1,0:T(8,128)(2,1)} custom-call(bf16[32,512,64]{2,1,0:T(8,128)(2,1)} %copy.37.msa_ref, s32[32,512]{1,0:T(8,128)} %mask_ref.1, f32[64,1]{1,0:T(8,128)} %copy.38.gamma_ref, f32[64,1]{1,0:T(8,128)} %copy.39.beta_ref, bf16[64,64]{1,0:T(8,128)(2,1)} %maximum_bitcast_fusion.weight_ref, f32[64,1]{1,0:T(8,128)} %copy.40.bias_ref), custom_call_target="tpu_custom_call" | custom-call | tf_op jit(solution)/shard_map/project/pallas_call | solution.py:41
  22.6 0.0 all-gather.3.cloned.1.call-update
  22.6 0.0 copy-done
  22.6 0.1 copy.41
  22.8 0.9 copy.42.weight_ref
  23.6 174.8 %all-gather.3.cloned.1.call-done = bf16[32,33,32,512]{3,2,1,0:T(8,128)(2,1)} async-done(((bf16[2,33,32,512]{3,2,1,0:T(8,128)(2,1)}), bf16[32,33,32,512]{3,2,1,0:T(8,128)(2,1)}) %all-gather.3.cloned.1.call-update) | async-done | bytes 34603024 | tf_op jit(solution)/shard_map/all_gather | solution.py:164
  198.4 7.3 %turn.1 = (bf16[128,32,512]{2,1,0:T(8,128)(2,1)}, bf16[128,512]{1,0:T(8,128)(2,1)}) custom-call(s32[1]{0:T(128)} %bitcast.row_ref, bf16[16,2,33,32,512]{4,3,2,1,0:T(8,128)(2,1)} %bitcast.16), custom_call_target="tpu_custom_call" | custom-call | tf_op jit(solution)/shard_map/turn/pallas_call | solution.py:80
  205.7 0.0 copy-done.3
  205.7 0.7 broadcast_in_dim.21.bias_ref
  206.4 103.0 %product.1 = f32[128,512,128]{2,1,0:T(8,128)} custom-call(bf16[128,32,512]{2,1,0:T(8,128)(2,1)} %get-tuple-element.7.left_ref, bf16[128,512]{1,0:T(8,128)(2,1)} %get-tuple-element.8.keep_ref, bf16[16,2,33,32,512]{4,3,2,1,0:T(8,128)(2,1)} %bitcast.17, bf16[128,1024]{1,0:T(8,128)(2,1)} %copy.42.weight_ref, f32[128,128]{1,0:T(8,128)} %broadcast_in_dim.21.bias_ref, ...), custom_call_target="tpu_custom_call" | custom-call | tf_op jit(solution)/shard_map/product/pallas_call | solution.py:131
  (1 shorter events, 0.0 us)
Async XLA Ops:
  6.5 8.9 %copy-start.1 = (bf16[64,32]{0,1:T(8,128)(2,1)S(1)}, bf16[64,32]{0,1:T(8,128)(2,1)}, u32[]{:S(2)}) copy-start(bf16[64,32]{0,1:T(8,128)(2,1)} %param.18) | copy-start | bytes 12292
  6.5 8.9 %copy-start.2 = (bf16[64,32]{0,1:T(8,128)(2,1)S(1)}, bf16[64,32]{0,1:T(8,128)(2,1)}, u32[]{:S(2)}) copy-start(bf16[64,32]{0,1:T(8,128)(2,1)} %param.16) | copy-start | bytes 12292
  6.5 191.9 %all-gather.3.cloned.1.call-start = ((), (), s32[]{:S(2)}) async-start(), calls=%async_computation | async-start | bytes 36765696 | tf_op jit(solution)/shard_map/all_gather | solution.py:164
  16.1 6.5 %copy-start = (bf16[1024,128]{1,0:T(8,128)(2,1)S(1)}, bf16[1024,128]{1,0:T(8,128)(2,1)}, u32[]{:S(2)}) copy-start(bf16[1024,128]{1,0:T(8,128)(2,1)} %param.20) | copy-start | bytes 786436
  198.4 7.3 %copy-start.3 = (bf16[128]{0:T(256)(128)(2,1)S(1)}, bf16[128]{0:T(256)(128)(2,1)}, u32[]{:S(2)}) copy-start(bf16[128]{0:T(256)(128)(2,1)} %param.21) | copy-start | bytes 772
Sparse Core Ops, SparseCore 0:
  22.8 175.6 all-gather.2

commit v2 on v1

v2 whole, which is shorter than its diff:
```python
import functools
import jax
import jax.numpy as jnp
from jax import lax
from jax.sharding import PartitionSpec as P
from jax.experimental import pallas as pl
from jax.experimental.pallas import tpu as pltpu

F32 = jnp.float32
BF16 = jnp.bfloat16
VMEM_LIMIT = 60 * 1024 * 1024
S_STEP = 16
I_STEP = 16
J_STEP = 128
MESH = pl.DeviceIdType.MESH
EARLY = 2


def project_kernel(msa_ref, mask_ref, gamma_ref, beta_ref, weight_ref, bias_ref, out_ref, tmp_ref):
    res, width = msa_ref.shape[1:]
    for s in range(S_STEP):
        x = msa_ref[s].astype(F32).T
        mean = jnp.sum(x, axis=0, keepdims=True) * (1.0 / width)
        centered = x - mean
        var = jnp.sum(centered * centered, axis=0, keepdims=True) * (1.0 / width)
        normed = centered * lax.rsqrt(var + 1e-5)
        normed = (normed * gamma_ref[...] + beta_ref[...]).astype(BF16)
        proj = jnp.dot(weight_ref[...], normed, preferred_element_type=F32) + bias_ref[...]
        tmp_ref[s] = proj * mask_ref[s:s + 1, :].astype(F32)
    half = out_ref.shape[2] - 1
    for g in range(2 * half // 8):
        flat = jnp.transpose(tmp_ref[:, g * 8:g * 8 + 8, :], (1, 0, 2)).astype(BF16)
        part, base = divmod(g * 8, half)
        for k in range(out_ref.shape[1]):
            out_ref[part, k, base:base + 8] = flat[:, :, k * J_STEP:(k + 1) * J_STEP]
    keep = mask_ref[...].astype(F32).astype(BF16)
    for k in range(out_ref.shape[1]):
        out_ref[0, k, half] = keep[:, k * J_STEP:(k + 1) * J_STEP]
        out_ref[1, k, half] = keep[:, k * J_STEP:(k + 1) * J_STEP]


def project(msa, mask, gamma, beta, weight, bias):
    seqs, res, width = msa.shape
    chans = weight.shape[0]
    return pl.pallas_call(
        project_kernel,
        grid=(seqs // S_STEP,),
        in_specs=[
            pl.BlockSpec((S_STEP, res, width), lambda g: (g, 0, 0)),
            pl.BlockSpec((S_STEP, res), lambda g: (g, 0)),
            pl.BlockSpec((width, 1), lambda g: (0, 0)),
            pl.BlockSpec((width, 1), lambda g: (0, 0)),
            pl.BlockSpec((chans, width), lambda g: (0, 0)),
            pl.BlockSpec((chans, 1), lambda g: (0, 0)),
        ],
        out_specs=pl.BlockSpec((2, res // J_STEP, chans // 2 + 1, S_STEP, J_STEP), lambda g: (0, 0, 0, g, 0)),
        out_shape=jax.ShapeDtypeStruct((2, res // J_STEP, chans // 2 + 1, seqs, J_STEP), BF16),
        scratch_shapes=[pltpu.VMEM((S_STEP, chans, res), F32)],
        compiler_params=pltpu.CompilerParams(vmem_limit_bytes=VMEM_LIMIT),
        name='project',
    )(msa, mask, gamma, beta, weight, bias)


def multiply(left, keep, right, weight, bias, outer_ref, scale_ref, emit):
    total = left.shape[-1]
    src, chans, seqs, cols = right.shape
    chans = chans - 1
    rows = left.shape[0] // chans
    count = jnp.dot(keep, right[:, chans].reshape(total, cols), preferred_element_type=F32)
    scale_ref[...] = 1.0 / (1e-3 + count)
    for g in range(chans // 4):
        slab = [right[:, g * 4 + k].reshape(total, cols) for k in range(4)]
        rhs = jnp.concatenate(slab, axis=1)
        for m in range(rows // 8):
            part = left[m * 8 * chans:(m + 1) * 8 * chans, :]
            prod = jnp.dot(part, rhs, preferred_element_type=F32).astype(BF16)
            for k in range(4):
                at = (g * 4 + k) * chans
                for i in range(8):
                    outer_ref[m * 4 + i // 2, at:at + chans, (i % 2) * cols:(i % 2 + 1) * cols] = (
                        prod[i * chans:(i + 1) * chans, k * cols:(k + 1) * cols])
    for h in range(rows // 2):
        lifted = jnp.dot(weight[...], outer_ref[h], preferred_element_type=F32)
        for k in range(2):
            part = lifted[:, k * cols:(k + 1) * cols] + bias[...]
            part = part * scale_ref[h * 2 + k:h * 2 + k + 1, :]
            emit(h * 2 + k, part.T)


def exchange_kernel(both, lift, bias, pair, x_out, bg, ag, left_out, keep_out,
                    left_vm, keep_vm, tmp, araw, bvm, outer, scale, pbuf, obuf, stage,
                    zs, zr, ys, yr, cs, cr, ss, sr, ls, asem, bsem, psem, osem, esem):
    z = lax.axis_index('seq')
    dap = lax.axis_index('dap')
    core = dap + 1 - 2 * lax.rem(dap, 2)
    far = lax.rem(dap + 2, 4)
    diag = lax.rem(core + 2, 4)
    me = z * 4 + dap
    blocks = both.shape[1]

    def remote(src, dst, send, recv, **target):
        return pltpu.make_async_remote_copy(src_ref=src, dst_ref=dst, send_sem=send, recv_sem=recv,
                                            device_id=target, device_id_type=MESH)

    def piece(item, plane):
        return ag.at[plane] if item == 1 else bg.at[max(item - 1, 0), plane * 4 + dap]

    def out_ok(way, h):
        return (z < 3) & (z >= h - 1) if way == 0 else (z > 0) & (z <= 4 - h)

    def in_ok(way, h):
        return z >= h if way == 0 else z + h <= 3

    def z_send(item, way, h):
        sign = 1 - 2 * way
        plane = z - sign * (h - 1)
        src = both.at[1, max(item - 1, 0)] if h == 1 and item != 1 else piece(item, plane)
        return remote(src, piece(item, plane), zs.at[way, item, h - 1], zr.at[way, item, h - 1], seq=z + sign)

    def z_land(item, way, h):
        sign = 1 - 2 * way
        at = piece(item, z - sign * h)
        return remote(at, at, zs.at[way, item, h - 1], zr.at[way, item, h - 1], seq=z - sign)

    def y_send(q, plane, own):
        at = bg.at[q, plane * 4 + dap]
        return remote(both.at[1, q] if own else at, at, ys.at[q, plane], yr.at[q, plane], dap=far)

    def y_land(q, plane):
        at = bg.at[q, plane * 4 + far]
        return remote(at, at, ys.at[q, plane], yr.at[q, plane], dap=far)

    def c_send(q, plane, which, own):
        at = bg.at[q, plane * 4 + (far if which else dap)]
        return remote(both.at[1, q] if own else at, at, cs.at[q, plane, which], cr.at[q, plane, which], dap=core)

    def c_land(q, plane, which):
        at = bg.at[q, plane * 4 + (diag if which else core)]
        return remote(at, at, cs.at[q, plane, which], cr.at[q, plane, which], dap=core)

    def begin(item):
        for way in range(2):
            @pl.when(out_ok(way, 1))
            def _():
                z_send(item, way, 1).start()
        if item != 1:
            q = max(item - 1, 0)
            y_send(q, z, True).start()
            c_send(q, z, 0, True).start()

    def arrive(item, h):
        for way in range(2):
            @pl.when(in_ok(way, h))
            def _():
                z_land(item, way, h).wait_recv()
            if h < 3:
                @pl.when(out_ok(way, h + 1))
                def _():
                    z_send(item, way, h + 1).start()
            if item != 1:
                @pl.when(in_ok(way, h))
                def _():
                    q = max(item - 1, 0)
                    plane = z - (1 - 2 * way) * h
                    y_send(q, plane, False).start()
                    c_send(q, plane, 0, False).start()

    def relay(q, h):
        if h == 0:
            y_land(q, z).wait_recv()
            c_send(q, z, 1, False).start()
        else:
            for way in range(2):
                @pl.when(in_ok(way, h))
                def _():
                    plane = z - (1 - 2 * way) * h
                    y_land(q, plane).wait_recv()
                    c_send(q, plane, 1, False).start()

    def settle(q):
        for plane in range(4):
            for which in range(2):
                c_land(q, plane, which).wait_recv()

    def turn(low, high):
        @pl.loop(0, 4)
        def _(plane):
            gap = jnp.abs(plane - z)

            @pl.when((gap >= low) & (gap <= high))
            def _():
                load = pltpu.make_async_copy(ag.at[plane], araw, asem)
                load.start()
                load.wait()
                lanes = pl.ds(pl.multiple_of(plane * 128, 128), 128)
                chans = araw.shape[1]
                for c in range(chans):
                    block = araw[:, c].reshape(128, 128).astype(F32).T
                    if c == chans - 1:
                        keep_vm[:, lanes] = block.astype(BF16)
                    else:
                        tmp[c] = block

                @pl.loop(0, 16)
                def _(k):
                    start = pl.multiple_of(k * 8, 8)
                    block = jnp.transpose(tmp[:, pl.ds(start, 8), :], (1, 0, 2)).reshape(256, 128)
                    row = pl.multiple_of(lax.rem(k, 2) * 256, 256)
                    left_vm[k // 2, pl.ds(row, 256), lanes] = block.astype(BF16)

    barrier = pltpu.get_barrier_semaphore()
    for other in (core, far, diag):
        pl.semaphore_signal(barrier, inc=1, device_id={'dap': other}, device_id_type=MESH)
    for way in range(2):
        @pl.when(out_ok(way, 1))
        def _():
            pl.semaphore_signal(barrier, inc=1, device_id={'seq': z + 1 - 2 * way}, device_id_type=MESH)
    inner = (z > 0) & (z < 3)

    @pl.when(inner)
    def _():
        pl.semaphore_wait(barrier, 5)

    @pl.when(jnp.logical_not(inner))
    def _():
        pl.semaphore_wait(barrier, 4)

    swaps = [remote(both.at[0, other], ag.at[z, dap], ss.at[k], sr.at[k], dap=other)
             for k, other in enumerate((core, far, diag))]
    for k in (1, 2, 0):
        swaps[k].start()
    begin(0)
    loads = [pltpu.make_async_copy(both.at[1, q], stage.at[q], ls.at[q]) for q in range(blocks)]
    loads.append(pltpu.make_async_copy(both.at[0, dap], stage.at[blocks], ls.at[blocks]))
    for load in loads:
        load.start()
    for load in loads:
        load.wait()
    puts = [pltpu.make_async_copy(stage.at[q], bg.at[q, me], ls.at[q]) for q in range(blocks)]
    puts.append(pltpu.make_async_copy(stage.at[blocks], ag.at[z, dap], ls.at[blocks]))
    for put in puts:
        put.start()
    for put in puts:
        put.wait()
    for k, other in enumerate((core, far, diag)):
        at = ag.at[z, other]
        remote(at, at, ss.at[k], sr.at[k], dap=other).wait_recv()
    begin(1)
    arrive(0, 1)
    relay(0, 0)
    arrive(0, 2)
    relay(0, 1)
    arrive(1, 1)
    begin(2)
    arrive(0, 3)
    relay(0, 2)
    turn(0, 1)
    arrive(1, 2)
    arrive(2, 1)
    begin(3)
    relay(0, 3)
    settle(0)
    first = pltpu.make_async_copy(bg.at[0], bvm.at[0], bsem.at[0])
    first.start()
    turn(2, 2)
    arrive(1, 3)
    turn(3, 3)
    first.wait()

    steps = EARLY * 8

    def pair_load(t):
        return pltpu.make_async_copy(pair.at[pl.ds(pl.multiple_of(lax.rem(t, 8) * I_STEP, I_STEP), I_STEP), t // 8],
                                     pbuf.at[lax.rem(t, 2)], psem.at[lax.rem(t, 2)])

    def out_put(t):
        return pltpu.make_async_copy(obuf.at[lax.rem(t, 2)],
                                     x_out.at[pl.ds(pl.multiple_of(lax.rem(t, 8) * I_STEP, I_STEP), I_STEP), t // 8],
                                     osem.at[lax.rem(t, 2)])

    exports = [pltpu.make_async_copy(left_vm, left_out, esem.at[0]), pltpu.make_async_copy(keep_vm, keep_out, esem.at[1])]
    for export in exports:
        export.start()
    pair_load(0).start()

    events = {
        0: lambda: relay(1, 0),
        1: lambda: (arrive(2, 2), relay(1, 1)),
        3: lambda: (arrive(3, 1), begin(4)),
        4: lambda: (arrive(2, 3), relay(1, 2)),
        6: lambda: (arrive(3, 2), relay(1, 3), relay(2, 0)),
        7: lambda: (settle(1), pltpu.make_async_copy(bg.at[1], bvm.at[1], bsem.at[1]).start()),
        8: lambda: (pltpu.make_async_copy(bg.at[1], bvm.at[1], bsem.at[1]).wait(), relay(2, 1)),
        9: lambda: arrive(4, 1),
        10: lambda: (arrive(3, 3), relay(2, 2)),
        12: lambda: (arrive(4, 2), relay(2, 3), relay(3, 0)),
        13: lambda: relay(3, 1),
        15: lambda: arrive(4, 3),
    }

    @pl.loop(0, steps)
    def _(t):
        for when, event in events.items():
            @pl.when(t == when)
            def _():
                event()

        @pl.when(t + 1 < steps)
        def _():
            pair_load(t + 1).start()
        pair_load(t).wait()

        @pl.when(t >= 2)
        def _():
            out_put(t - 2).wait()
        slot = lax.rem(t, 2)
        group = lax.rem(t, 8)

        def emit(i, value):
            obuf[slot, i] = pbuf[slot, i] + value

        multiply(left_vm.at[group], keep_vm[pl.ds(pl.multiple_of(group * I_STEP, I_STEP), I_STEP), :], bvm.at[t // 8],
                 lift, bias, outer, scale, emit)
        out_put(t).start()

    relay(3, 2)
    relay(3, 3)
    settle(2)
    settle(3)
    out_put(steps - 2).wait()
    out_put(steps - 1).wait()
    for export in exports:
        export.wait()
    for swap in swaps:
        swap.wait_send()
    for item in range(blocks + 1):
        for h in range(1, 4):
            for way in range(2):
                @pl.when(out_ok(way, h))
                def _():
                    z_send(item, way, h).wait_send()
    for q in range(blocks):
        for plane in range(4):
            y_send(q, plane, False).wait_send()
            for which in range(2):
                c_send(q, plane, which, False).wait_send()


def exchange(both, lift, bias, pair):
    _, blocks, chans, seqs, cols = both.shape
    rows, _, _, width = pair.shape
    src = 16
    total = src * seqs
    vmem = pl.BlockSpec(memory_space=pltpu.VMEM)
    hbm = pl.BlockSpec(memory_space=pl.ANY)
    dma = pltpu.SemaphoreType.DMA
    groups = rows // I_STEP
    hidden = chans - 1
    return pl.pallas_call(
        exchange_kernel,
        in_specs=[hbm, vmem, vmem, hbm],
        out_specs=[hbm] * 5,
        out_shape=[
            jax.ShapeDtypeStruct((rows, EARLY, cols, width), F32),
            jax.ShapeDtypeStruct((blocks, src, chans, seqs, cols), BF16),
            jax.ShapeDtypeStruct((4, 4, chans, seqs, cols), BF16),
            jax.ShapeDtypeStruct((groups, I_STEP * hidden, total), BF16),
            jax.ShapeDtypeStruct((rows, total), BF16),
        ],
        scratch_shapes=[
            pltpu.VMEM((groups, I_STEP * hidden, total), BF16),
            pltpu.VMEM((rows, total), BF16),
            pltpu.VMEM((hidden, rows, 4 * seqs), F32),
            pltpu.VMEM((4, chans, seqs, cols), BF16),
            pltpu.VMEM((2, src, chans, seqs, cols), BF16),
            pltpu.VMEM((I_STEP // 2, hidden * hidden, 2 * cols), BF16),
            pltpu.VMEM((I_STEP, cols), F32),
            pltpu.VMEM((2, I_STEP, cols, width), F32),
            pltpu.VMEM((2, I_STEP, cols, width), F32),
            pltpu.VMEM((blocks + 1, chans, seqs, cols), BF16),
            dma((2, 5, 3)), dma((2, 5, 3)), dma((4, 4)), dma((4, 4)), dma((4, 4, 2)), dma((4, 4, 2)),
            dma((3,)), dma((3,)), dma((5,)), dma, dma((2,)), dma((2,)), dma((2,)), dma((2,)),
        ],
        compiler_params=pltpu.CompilerParams(vmem_limit_bytes=VMEM_LIMIT, collective_id=0, has_side_effects=True),
        name='exchange',
    )(both, lift, bias, pair)


def finish_kernel(left_ref, keep_ref, right_ref, weight_ref, bias_ref, pair_ref, early_ref, out_ref, outer_ref, scale_ref):
    out_ref[:, 0] = early_ref[...]

    def emit(i, value):
        out_ref[i, 1] = pair_ref[i] + value

    multiply(left_ref, keep_ref[...], right_ref, weight_ref, bias_ref, outer_ref, scale_ref, emit)


def finish(left, keep, right, weight, bias, pair, early):
    groups, depth, total = left.shape
    blocks, src, chans, seqs, cols = right.shape
    rows, _, _, width = pair.shape
    hidden = chans - 1
    pair = pair.reshape(rows, 2, EARLY, cols, width)
    out = pl.pallas_call(
        finish_kernel,
        grid=(blocks - EARLY, groups),
        in_specs=[
            pl.BlockSpec((None, depth, total), lambda q, g: (g, 0, 0)),
            pl.BlockSpec((I_STEP, total), lambda q, g: (g, 0)),
            pl.BlockSpec((None, src, chans, seqs, cols), lambda q, g: (q + EARLY, 0, 0, 0, 0)),
            pl.BlockSpec(weight.shape, lambda q, g: (0, 0)),
            pl.BlockSpec(bias.shape, lambda q, g: (0, 0)),
            pl.BlockSpec((I_STEP, None, None, cols, width), lambda q, g: (g, 1, q, 0, 0)),
            pl.BlockSpec((I_STEP, None, cols, width), lambda q, g: (g, q, 0, 0)),
        ],
        out_specs=pl.BlockSpec((I_STEP, 2, None, cols, width), lambda q, g: (g, 0, q, 0, 0)),
        out_shape=jax.ShapeDtypeStruct(pair.shape, F32),
        scratch_shapes=[pltpu.VMEM((I_STEP // 2, hidden * hidden, 2 * cols), BF16), pltpu.VMEM((I_STEP, cols), F32)],
        compiler_params=pltpu.CompilerParams(vmem_limit_bytes=VMEM_LIMIT),
        name='finish',
    )(left, keep, right, weight, bias, pair, early)
    return out.reshape(rows, blocks * cols, width)


def solution(mesh):
    msa_spec = P(('data', 'seq', 'dap'), None, None)
    mask_spec = P(('data', 'seq', 'dap'), None)
    pair_spec = P(('data', 'dap'), None, None)

    def device_step(msa, mask, pair, ln_gamma, ln_beta, w_a, b_a, w_b, b_b, w_out, b_out):
        hidden = w_a.shape[1]
        width = w_out.shape[1]
        res = msa.shape[1]
        weight = jnp.concatenate([w_a, w_b], axis=1).T
        bias = jnp.concatenate([b_a, b_b]).astype(F32)[:, None]
        both = project(msa, mask, ln_gamma.astype(F32)[:, None], ln_beta.astype(F32)[:, None], weight, bias)
        lift = w_out.reshape(hidden, hidden, width).transpose(2, 1, 0).reshape(width, hidden * hidden)
        bias_col = jnp.broadcast_to(b_out.astype(F32)[:, None], (width, J_STEP))
        tiled = pair.reshape(pair.shape[0], res // J_STEP, J_STEP, width)
        early, right, _, left, keep = exchange(both, lift, bias_col, tiled)
        return finish(left, keep, right, lift, bias_col, tiled, early)

    return jax.shard_map(device_step, mesh=mesh, in_specs=(msa_spec, mask_spec, pair_spec, P(), P(), P(), P(), P(), P(), P(), P()), out_specs=pair_spec, check_vma=False)
```

time: 317 us -> 261 us (0.82)
  waiting for transfers between devices: 175 us -> 0 us
  Pallas kernels: 117 us -> 247 us
  between operations: 13.4 us -> 0.02 us
    all_gather x1 -> x0, waiting for transfers between devices: 175 us -> none  [device_step(): gathered = lax.all_gather(both, ('seq', 'dap'))]
    pallas_call x2, Pallas kernels: 110 us -> 240 us  [the longest x1 184 us: exchange(): pl.pallas_call(exchange_kernel, in_specs=[hbm, vmem, vmem, hbm], out_spec...]
  transfers between devices with their start and end apart: 1 -> 0, of which waited for: 1 -> 0; matrix products, arithmetic and copies ran while one was open for 0% -> 0% of each run, Pallas kernels for 0% -> 0%
where the time goes in v2:
time: 261 us; the launch traced here: 260 us
  Pallas kernels  247 us (95%)
  local copies, waits for them, and re-layouts  10.1 us (4%)
  other arithmetic  3.38 us (1%)
    pallas_call x1, Pallas kernels, exchange(): pl.pallas_call(exchange_kernel, in_specs=[hbm, vmem, vmem, hbm], out_spec...  184 us
    pallas_call x1, Pallas kernels, finish(): pl.pallas_call(finish_kernel, grid=(blocks - EARLY, groups), in_specs=[pl...  55.7 us
    pallas_call x1, Pallas kernels, project(): pl.pallas_call(project_kernel, grid=(seqs // S_STEP,), in_specs=[pl.Block...  6.51 us

profile of v2, /device:TPU:0, one launch (start us, length us, event | category | flops | bytes accessed | tf_op | source)
XLA Modules:
  0.0 260.2 jit_solution(1221923497327663726)
XLA Ops:
  0.0 0.7 bitcast_convert_fusion.1
  0.7 0.7 bitcast_convert_fusion
  1.3 0.7 maximum_convert_fusion
  2.1 1.3 maximum_bitcast_fusion.weight_ref
  3.4 0.7 copy.43.bias_ref
  4.1 0.7 copy.42.beta_ref
  4.8 0.7 copy.41.gamma_ref
  5.5 1.4 broadcast_in_dim.21.bias.bias_ref
  6.8 1.1 copy.44
  7.9 0.9 copy.45.lift.weight_ref
  8.8 4.7 %copy.40.msa_ref = bf16[32,512,64]{2,1,0:T(8,128)(2,1)} copy(bf16[32,512,64]{1,2,0:T(8,128)(2,1)} %param.11) | data formatting | bytes 4194304 | tf_op args[0]
  13.5 6.5 %project.1.both = bf16[2,4,33,32,128]{4,3,2,1,0:T(8,128)(2,1)} custom-call(bf16[32,512,64]{2,1,0:T(8,128)(2,1)} %copy.40.msa_ref, s32[32,512]{1,0:T(8,128)} %mask_ref.1, f32[64,1]{1,0:T(8,128)} %copy.41.gamma_ref, f32[64,1]{1,0:T(8,128)} %copy.42.beta_ref, bf16[64,64]{1,0:T(8,128)(2,1)} %maximum_bitcast_fusion.weight_ref, f32[64,1]{1,0:T(8,128)} %copy.43.bias_ref), custom_call_target="tpu_custom_call" | custom-call | tf_op jit(solution)/shard_map/project/pallas_call | solution.py:45
  20.0 184.4 %exchange.1 = (f32[128,2,128,128]{3,2,1,0:T(8,128)}, bf16[4,16,33,32,128]{4,3,2,1,0:T(8,128)(2,1)}, bf16[4,4,33,32,128]{4,3,2,1,0:T(8,128)(2,1)}, bf16[8,512,512]{2,1,0:T(8,128)(2,1)}, bf16[128,512]{1,0:T(8,128)(2,1)}) custom-call(bf16[2,4,33,32,128]{4,3,2,1,0:T(8,128)(2,1)} %project.1.both, bf16[128,1024]{1,0:T(8,128)(2,1)} %copy.45.lift.weight_ref, ...), custom_call_target="tpu_custom_call" | custom-call | tf_op jit(solution)/shard_map/exchange/pallas_call | solution.py:359
  204.4 55.7 %finish.1 = f32[128,2,2,128,128]{4,3,2,1,0:T(8,128)} custom-call(bf16[8,512,512]{2,1,0:T(8,128)(2,1)} %get-tuple-element.9.left_ref, bf16[128,512]{1,0:T(8,128)(2,1)} %get-tuple-element.10.keep_ref, bf16[4,16,33,32,128]{4,3,2,1,0:T(8,128)(2,1)} %get-tuple-element.11.right_ref, bf16[128,1024]{1,0:T(8,128)(2,1)} %copy.45.lift.weight_ref, ...), custom_call_target="tpu_custom_call" | custom-call | tf_op jit(solution)/shard_map/finish/pallas_call | solution.py:404

commit v3 on v2

v3 whole, which is shorter than its diff:
```python
import functools
import jax
import jax.numpy as jnp
from jax import lax
from jax.sharding import PartitionSpec as P
from jax.experimental import pallas as pl
from jax.experimental.pallas import tpu as pltpu

F32 = jnp.float32
BF16 = jnp.bfloat16
VMEM_LIMIT = 60 * 1024 * 1024
S_STEP = 16
I_STEP = 16
J_STEP = 128
MESH = pl.DeviceIdType.MESH
ITEMS = ('b0', 'b1', 'a0', 'a1', 'a2', 'b2', 'b3', 'a3')
EARLY = 2


def project_kernel(msa_ref, mask_ref, vec_ref, weight_ref, out_ref, tmp_ref):
    width = msa_ref.shape[1]
    for s in range(S_STEP):
        x = msa_ref[s].astype(F32)
        mean = jnp.sum(x, axis=0, keepdims=True) * (1.0 / width)
        centered = x - mean
        var = jnp.sum(centered * centered, axis=0, keepdims=True) * (1.0 / width)
        normed = centered * lax.rsqrt(var + 1e-5)
        normed = (normed * vec_ref[:, 0:1] + vec_ref[:, 1:2]).astype(BF16)
        proj = jnp.dot(weight_ref[...], normed, preferred_element_type=F32) + vec_ref[:, 2:3]
        tmp_ref[s] = proj * mask_ref[s:s + 1, :].astype(F32)
    half = out_ref.shape[2] - 1
    for g in range(2 * half // 8):
        flat = jnp.transpose(tmp_ref[:, g * 8:g * 8 + 8, :], (1, 0, 2)).astype(BF16)
        part, base = divmod(g * 8, half)
        for k in range(out_ref.shape[1]):
            out_ref[part, k, base:base + 8] = flat[:, :, k * J_STEP:(k + 1) * J_STEP]
    keep = mask_ref[...].astype(F32).astype(BF16)
    for k in range(out_ref.shape[1]):
        out_ref[0, k, half] = keep[:, k * J_STEP:(k + 1) * J_STEP]
        out_ref[1, k, half] = keep[:, k * J_STEP:(k + 1) * J_STEP]


def project(msa, mask, vec, weight):
    seqs, width, res = msa.shape
    chans = weight.shape[0]
    return pl.pallas_call(
        project_kernel,
        grid=(seqs // S_STEP,),
        in_specs=[
            pl.BlockSpec((S_STEP, width, res), lambda g: (g, 0, 0)),
            pl.BlockSpec((S_STEP, res), lambda g: (g, 0)),
            pl.BlockSpec((width, 3), lambda g: (0, 0)),
            pl.BlockSpec((chans, width), lambda g: (0, 0)),
        ],
        out_specs=pl.BlockSpec((2, res // J_STEP, chans // 2 + 1, S_STEP, J_STEP), lambda g: (0, 0, 0, g, 0)),
        out_shape=jax.ShapeDtypeStruct((2, res // J_STEP, chans // 2 + 1, seqs, J_STEP), BF16),
        scratch_shapes=[pltpu.VMEM((S_STEP, chans, res), F32)],
        compiler_params=pltpu.CompilerParams(vmem_limit_bytes=VMEM_LIMIT),
        name='project',
    )(msa, mask, vec, weight)


def multiply(left, spot, right, weight, bias, outer_ref, scale_ref, emit):
    src, chans, seqs, cols = right.shape
    chans = chans - 1
    total = src * seqs
    rows = I_STEP

    def rows_of(start, size):
        return jnp.concatenate([left[p, pl.ds(start, size), :] for p in range(left.shape[0])], axis=1)

    base = pl.multiple_of(spot * (rows * chans), rows * chans)
    keep = rows_of(pl.multiple_of(2 * rows * chans + spot * rows, rows), rows)
    count = jnp.dot(keep, right[:, chans].reshape(total, cols), preferred_element_type=F32)
    scale_ref[...] = 1.0 / (1e-3 + count)
    for g in range(chans // 4):
        slab = [right[:, g * 4 + k].reshape(total, cols) for k in range(4)]
        rhs = jnp.concatenate(slab, axis=1)
        for m in range(rows // 8):
            part = rows_of(pl.multiple_of(base + m * 8 * chans, 8 * chans), 8 * chans)
            prod = jnp.dot(part, rhs, preferred_element_type=F32).astype(BF16)
            for k in range(4):
                at = (g * 4 + k) * chans
                for i in range(8):
                    outer_ref[m * 4 + i // 2, at:at + chans, (i % 2) * cols:(i % 2 + 1) * cols] = (
                        prod[i * chans:(i + 1) * chans, k * cols:(k + 1) * cols])
    for h in range(rows // 2):
        lifted = jnp.dot(weight[...], outer_ref[h], preferred_element_type=F32)
        for k in range(2):
            part = lifted[:, k * cols:(k + 1) * cols] + bias[...]
            part = part * scale_ref[h * 2 + k:h * 2 + k + 1, :]
            emit(h * 2 + k, part.T)


def exchange_kernel(both, lift, bias, pair, x_out, right_out, left_out,
                    left_vm, right_vm, tmp, araw, outer, scale, pbuf, obuf,
                    zs, zr, ys, yr, cs, cr, ss, sr, ls, psem, osem, esem):
    z = lax.axis_index('seq')
    dap = lax.axis_index('dap')
    core = dap + 1 - 2 * lax.rem(dap, 2)
    far = lax.rem(dap + 2, 4)
    diag = lax.rem(core + 2, 4)
    me = z * 4 + dap
    blocks = both.shape[1]

    def remote(src, dst, send, recv, **target):
        return pltpu.make_async_remote_copy(src_ref=src, dst_ref=dst, send_sem=send, recv_sem=recv,
                                            device_id=target, device_id_type=MESH)

    def piece(item, plane):
        kind, at = ITEMS[item][0], int(ITEMS[item][1])
        return left_vm.at[at, plane] if kind == 'a' else right_vm.at[at, plane * 4 + dap]

    def out_ok(way, h):
        return (z < 3) & (z >= h - 1) if way == 0 else (z > 0) & (z <= 4 - h)

    def in_ok(way, h):
        return z >= h if way == 0 else z + h <= 3

    def z_send(item, way, h):
        sign = 1 - 2 * way
        at = piece(item, z - sign * (h - 1))
        return remote(at, at, zs.at[way, item, h - 1], zr.at[way, item, h - 1], seq=z + sign)

    def z_land(item, way, h):
        sign = 1 - 2 * way
        at = piece(item, z - sign * h)
        return remote(at, at, zs.at[way, item, h - 1], zr.at[way, item, h - 1], seq=z - sign)

    def y_copy(q, plane, owner):
        at = right_vm.at[q, plane * 4 + owner]
        return remote(at, at, ys.at[q, plane], yr.at[q, plane], dap=far)

    def c_copy(q, plane, which, owner):
        at = right_vm.at[q, plane * 4 + owner]
        return remote(at, at, cs.at[q, plane, which], cr.at[q, plane, which], dap=core)

    def begin(item):
        for way in range(2):
            @pl.when(out_ok(way, 1))
            def _():
                if item > 0:
                    z_send(item - 1, way, 1).wait_send()
                z_send(item, way, 1).start()
        if ITEMS[item][0] == 'b':
            q = int(ITEMS[item][1])
            y_copy(q, z, dap).start()
            c_copy(q, z, 0, dap).start()

    def early(item, *hops):
        for h in hops:
            for way in range(2):
                @pl.when(in_ok(way, h) & out_ok(way, h + 1))
                def _():
                    z_land(item, way, h).wait_recv()
                    z_send(item, way, h + 1).start()

    def late(item, *hops):
        for h in hops:
            for way in range(2):
                end = z == (3 if way == 0 else 0)

                @pl.when(in_ok(way, h) & end)
                def _():
                    z_land(item, way, h).wait_recv()

                if ITEMS[item][0] == 'b':
                    @pl.when(in_ok(way, h))
                    def _():
                        q = int(ITEMS[item][1])
                        plane = z - (1 - 2 * way) * h
                        y_copy(q, plane, dap).start()
                        c_copy(q, plane, 0, dap).start()

    def relay(q, *hops):
        for h in hops:
            if h == 0:
                y_copy(q, z, far).wait_recv()
                c_copy(q, z, 1, far).start()
            else:
                for way in range(2):
                    @pl.when(in_ok(way, h))
                    def _():
                        plane = z - (1 - 2 * way) * h
                        y_copy(q, plane, far).wait_recv()
                        c_copy(q, plane, 1, far).start()

    def export(q):
        return pltpu.make_async_copy(right_vm.at[q], right_out.at[q - EARLY], esem.at[q])

    def settle(q):
        for plane in range(4):
            for which, owner in enumerate((core, diag)):
                c_copy(q, plane, which, owner).wait_recv()
        if q >= EARLY:
            export(q).start()

    def turn():
        chans = araw.shape[1]
        for c in range(chans):
            block = araw[:, c].reshape(128, 128).astype(F32).T
            if c == chans - 1:
                for r in range(blocks):
                    left_vm[r, z, 1024:1056, :] = block[r * 32:(r + 1) * 32].astype(BF16)
            else:
                tmp[c] = block

        @pl.loop(0, 16)
        def _(k):
            start = pl.multiple_of(k * 8, 8)
            block = jnp.transpose(tmp[:, pl.ds(start, 8), :], (1, 0, 2)).reshape(256, 128)
            row = pl.multiple_of(lax.rem(k, 4) * 256, 256)
            left_vm[k // 4, z, pl.ds(row, 256), :] = block.astype(BF16)

    barrier = pltpu.get_barrier_semaphore()
    for other in (core, far, diag):
        pl.semaphore_signal(barrier, inc=1, device_id={'dap': other}, device_id_type=MESH)
    for way in range(2):
        @pl.when(out_ok(way, 1))
        def _():
            pl.semaphore_signal(barrier, inc=1, device_id={'seq': z + 1 - 2 * way}, device_id_type=MESH)
    inner = (z > 0) & (z < 3)
    loads = [pltpu.make_async_copy(both.at[1, q], right_vm.at[q, me], ls.at[q]) for q in range(blocks)]
    loads.append(pltpu.make_async_copy(both.at[0, dap], araw.at[dap], ls.at[blocks]))
    for load in loads:
        load.start()

    @pl.when(inner)
    def _():
        pl.semaphore_wait(barrier, 5)

    @pl.when(jnp.logical_not(inner))
    def _():
        pl.semaphore_wait(barrier, 4)

    swaps = [remote(both.at[0, other], araw.at[dap], ss.at[k], sr.at[k], dap=other)
             for k, other in enumerate((core, far, diag))]
    for k in (1, 2, 0):
        swaps[k].start()
    for load in loads:
        load.wait()
    begin(0)
    for k, other in enumerate((core, far, diag)):
        remote(araw.at[other], araw.at[other], ss.at[k], sr.at[k], dap=other).wait_recv()
    begin(1)
    turn()
    early(0, 1, 2)
    begin(2)
    late(0, 1, 2)
    relay(0, 0, 1)
    early(1, 1, 2)
    begin(3)
    late(0, 3)
    relay(0, 2, 3)
    late(1, 1, 2)
    relay(1, 0, 1)
    early(2, 1, 2)
    begin(4)
    late(1, 3)
    relay(1, 2, 3)
    settle(0)
    settle(1)
    late(2, 1, 2, 3)

    steps = 8 * EARLY
    final = pltpu.make_async_copy(left_vm, left_out, esem.at[blocks])

    def part(t):
        return t // (2 * EARLY)

    def col(t):
        return lax.rem(t, 2 * EARLY) // 2

    def tile(t):
        row = (part(t) * 2 + lax.rem(t, 2)) * I_STEP
        return pl.ds(pl.multiple_of(row, I_STEP), I_STEP), col(t)

    def pair_load(t):
        slot = lax.rem(t, 2)
        return pltpu.make_async_copy(pair.at[tile(t)], pbuf.at[slot], psem.at[slot])

    def out_put(t):
        slot = lax.rem(t, 2)
        return pltpu.make_async_copy(obuf.at[slot], x_out.at[tile(t)], osem.at[slot])

    pair_load(jnp.int32(0)).start()
    events = {
        0: lambda: early(3, 1),
        2: lambda: (early(3, 2), begin(5)),
        4: lambda: (late(3, 1, 2, 3), early(4, 1)),
        6: lambda: (early(4, 2), begin(6)),
        8: lambda: (late(4, 1, 2, 3), early(5, 1), late(5, 1)),
        9: lambda: (begin(7), relay(2, 0)),
        10: lambda: (early(5, 2), late(5, 2), early(6, 1), relay(2, 1)),
        11: lambda: late(6, 1),
        12: lambda: (early(6, 2), late(5, 3), late(6, 2), early(7, 1), relay(2, 2), relay(3, 0), early(7, 2),
                     late(6, 3), relay(2, 3), settle(2), relay(3, 1), late(7, 1, 2, 3), final.start()),
        13: lambda: relay(3, 2),
        14: lambda: (relay(3, 3), settle(3)),
    }

    @pl.loop(0, steps)
    def _(t):
        for when, event in events.items():
            @pl.when(t == when)
            def _():
                event()

        @pl.when(t + 1 < steps)
        def _():
            pair_load(t + 1).start()
        pair_load(t).wait()

        @pl.when(t >= 2)
        def _():
            out_put(t - 2).wait()
        slot = lax.rem(t, 2)

        def emit(i, value):
            obuf[slot, i] = pbuf[slot, i] + value

        multiply(left_vm.at[part(t)], lax.rem(t, 2), right_vm.at[col(t)], lift, bias, outer, scale, emit)
        out_put(t).start()

    out_put(jnp.int32(steps - 2)).wait()
    out_put(jnp.int32(steps - 1)).wait()
    for q in range(EARLY, blocks):
        export(q).wait()
    final.wait()
    for swap in swaps:
        swap.wait_send()
    for item in range(len(ITEMS)):
        for h in range(1 if item == len(ITEMS) - 1 else 2, 4):
            for way in range(2):
                @pl.when(out_ok(way, h))
                def _():
                    z_send(item, way, h).wait_send()
    for q in range(blocks):
        for plane in range(4):
            y_copy(q, plane, dap).wait_send()
            for which, owner in enumerate((dap, far)):
                c_copy(q, plane, which, owner).wait_send()


def exchange(both, lift, bias, pair):
    _, blocks, chans, seqs, cols = both.shape
    rows, _, _, width = pair.shape
    src = 16
    vmem = pl.BlockSpec(memory_space=pltpu.VMEM)
    hbm = pl.BlockSpec(memory_space=pl.ANY)
    dma = pltpu.SemaphoreType.DMA
    hidden = chans - 1
    part = rows // blocks
    left_shape = (4, part * hidden + part, 4 * seqs)
    return pl.pallas_call(
        exchange_kernel,
        in_specs=[hbm, vmem, vmem, hbm],
        out_specs=[hbm] * 3,
        out_shape=[
            jax.ShapeDtypeStruct((rows, EARLY, cols, width), F32),
            jax.ShapeDtypeStruct((blocks - EARLY, src, chans, seqs, cols), BF16),
            jax.ShapeDtypeStruct((blocks,) + left_shape, BF16),
        ],
        scratch_shapes=[
            pltpu.VMEM((blocks,) + left_shape, BF16),
            pltpu.VMEM((blocks, src, chans, seqs, cols), BF16),
            pltpu.VMEM((hidden, rows, 4 * seqs), F32),
            pltpu.VMEM((4, chans, seqs, cols), BF16),
            pltpu.VMEM((I_STEP // 2, hidden * hidden, 2 * cols), BF16),
            pltpu.VMEM((I_STEP, cols), F32),
            pltpu.VMEM((2, I_STEP, cols, width), F32),
            pltpu.VMEM((2, I_STEP, cols, width), F32),
            dma((2, 8, 3)), dma((2, 8, 3)), dma((4, 4)), dma((4, 4)), dma((4, 4, 2)), dma((4, 4, 2)),
            dma((3,)), dma((3,)), dma((5,)), dma((2,)), dma((2,)), dma((5,)),
        ],
        compiler_params=pltpu.CompilerParams(vmem_limit_bytes=VMEM_LIMIT, collective_id=0, has_side_effects=True),
        name='exchange',
    )(both, lift, bias, pair)


def finish_kernel(left_ref, right_ref, weight_ref, bias_ref, pair_ref, early_ref, out_ref, outer_ref, scale_ref):
    out_ref[:, 0] = early_ref[...]

    def emit(i, value):
        out_ref[i, 1] = pair_ref[i] + value

    multiply(left_ref, lax.rem(pl.program_id(1), 2), right_ref, weight_ref, bias_ref, outer_ref, scale_ref, emit)


def finish(left, right, weight, bias, pair, early):
    rest, src, chans, seqs, cols = right.shape
    rows, blocks, _, width = pair.shape
    hidden = chans - 1
    pair = pair.reshape(rows, 2, EARLY, cols, width)
    out = pl.pallas_call(
        finish_kernel,
        grid=(rest, rows // I_STEP),
        in_specs=[
            pl.BlockSpec((None,) + left.shape[1:], lambda q, g: (g // 2, 0, 0, 0)),
            pl.BlockSpec((None, src, chans, seqs, cols), lambda q, g: (q, 0, 0, 0, 0)),
            pl.BlockSpec(weight.shape, lambda q, g: (0, 0)),
            pl.BlockSpec(bias.shape, lambda q, g: (0, 0)),
            pl.BlockSpec((I_STEP, None, None, cols, width), lambda q, g: (g, 1, q, 0, 0)),
            pl.BlockSpec((I_STEP, None, cols, width), lambda q, g: (g, q, 0, 0)),
        ],
        out_specs=pl.BlockSpec((I_STEP, 2, None, cols, width), lambda q, g: (g, 0, q, 0, 0)),
        out_shape=jax.ShapeDtypeStruct(pair.shape, F32),
        scratch_shapes=[pltpu.VMEM((I_STEP // 2, hidden * hidden, 2 * cols), BF16), pltpu.VMEM((I_STEP, cols), F32)],
        compiler_params=pltpu.CompilerParams(vmem_limit_bytes=VMEM_LIMIT),
        name='finish',
    )(left, right, weight, bias, pair, early)
    return out.reshape(rows, blocks * cols, width)


def solution(mesh):
    msa_spec = P(('data', 'seq', 'dap'), None, None)
    mask_spec = P(('data', 'seq', 'dap'), None)
    pair_spec = P(('data', 'dap'), None, None)

    def device_step(msa, mask, pair, ln_gamma, ln_beta, w_a, b_a, w_b, b_b, w_out, b_out):
        hidden = w_a.shape[1]
        width = w_out.shape[1]
        res = msa.shape[1]
        weight = jnp.concatenate([w_a.T, w_b.T], axis=0)
        vec = jnp.stack([ln_gamma, ln_beta, jnp.concatenate([b_a, b_b])], axis=1).astype(F32)
        both = project(msa.transpose(0, 2, 1), mask, vec, weight)
        lift = w_out.reshape(hidden, hidden, width).transpose(2, 1, 0).reshape(width, hidden * hidden)
        bias_col = jnp.broadcast_to(b_out.astype(F32)[:, None], (width, J_STEP))
        tiled = pair.reshape(pair.shape[0], res // J_STEP, J_STEP, width)
        early, right, left = exchange(both, lift, bias_col, tiled)
        return finish(left, right, lift, bias_col, tiled, early)

    return jax.shard_map(device_step, mesh=mesh, in_specs=(msa_spec, mask_spec, pair_spec, P(), P(), P(), P(), P(), P(), P(), P()), out_specs=pair_spec, check_vma=False)
```

time: 261 us -> 248 us (0.950)
  Pallas kernels: 247 us -> 240 us
  local copies, waits for them, and re-layouts: 10.1 us -> 3.99 us
    pallas_call x1, Pallas kernels: 184 us -> 178 us  [exchange(): pl.pallas_call(exchange_kernel, in_specs=[hbm, vmem, vmem, hbm], out_spec...]
    unnamed x1 -> x0, local copies, waits for them, and re-layouts: 4.75 us -> none
where the time goes in v3:
time: 248 us; the launch traced here: 247 us
  Pallas kernels  240 us (97%)
  local copies, waits for them, and re-layouts  3.99 us (2%)
  other arithmetic  2.75 us (1%)
    pallas_call x1, Pallas kernels, exchange(): pl.pallas_call(exchange_kernel, in_specs=[hbm, vmem, vmem, hbm], out_spec...  178 us
    pallas_call x1, Pallas kernels, finish(): pl.pallas_call(finish_kernel, grid=(rest, rows // I_STEP), in_specs=[pl.B...  57 us
    pallas_call x1, Pallas kernels, project(): pl.pallas_call(project_kernel, grid=(seqs // S_STEP,), in_specs=[pl.Block...  5.52 us

profile of v3, /device:TPU:0, one launch (start us, length us, event | category | flops | bytes accessed | tf_op | source)
XLA Modules:
  0.0 247.1 jit_solution(2724678104917430397)
XLA Ops:
  0.0 0.7 maximum_bitcast_fusion
  0.7 0.7 maximum_convert_fusion
  1.4 1.3 pad_maximum_fusion.weight_ref
  2.8 0.7 copy.31.vec_ref
  3.5 1.4 broadcast_in_dim.2.bias.bias_ref
  4.8 1.1 copy.32
  5.9 0.9 copy.33.lift.weight_ref
  6.7 5.5 %project.1.both = bf16[2,4,33,32,128]{4,3,2,1,0:T(8,128)(2,1)} custom-call(bf16[32,64,512]{2,1,0:T(8,128)(2,1)} %bitcast.16, s32[32,512]{1,0:T(8,128)} %mask_ref.1, f32[64,3]{1,0:T(8,128)} %copy.31.vec_ref, bf16[64,64]{1,0:T(8,128)(2,1)} %pad_maximum_fusion.weight_ref), custom_call_target="tpu_custom_call" | custom-call | tf_op jit(solution)/shard_map/project/pallas_call | solution.py:46
  12.3 177.9 %exchange.1 = (f32[128,2,128,128]{3,2,1,0:T(8,128)}, bf16[2,16,33,32,128]{4,3,2,1,0:T(8,128)(2,1)}, bf16[4,4,1056,128]{3,2,1,0:T(8,128)(2,1)}) custom-call(bf16[2,4,33,32,128]{4,3,2,1,0:T(8,128)(2,1)} %project.1.both, bf16[128,1024]{1,0:T(8,128)(2,1)} %copy.33.lift.weight_ref, f32[128,128]{1,0:T(8,128)} %broadcast_in_dim.2.bias.bias_ref, ...), custom_call_target="tpu_custom_call" | custom-call | tf_op jit(solution)/shard_map/exchange/pallas_call | solution.py:355
  190.2 57.0 %finish.1 = f32[128,2,2,128,128]{4,3,2,1,0:T(8,128)} custom-call(bf16[4,4,1056,128]{3,2,1,0:T(8,128)(2,1)} %get-tuple-element.8.left_ref, bf16[2,16,33,32,128]{4,3,2,1,0:T(8,128)(2,1)} %get-tuple-element.9.right_ref, bf16[128,1024]{1,0:T(8,128)(2,1)} %copy.33.lift.weight_ref, f32[128,128]{1,0:T(8,128)} %broadcast_in_dim.2.bias.bias_ref, ...), custom_call_target="tpu_custom_call" | custom-call | tf_op jit(solution)/shard_map/finish/pallas_call | solution.py:395

commit v4 on v3

--- a/solution.py
+++ b/solution.py
@@ -73,6 +73,7 @@
     keep = rows_of(pl.multiple_of(2 * rows * chans + spot * rows, rows), rows)
     count = jnp.dot(keep, right[:, chans].reshape(total, cols), preferred_element_type=F32)
     scale_ref[...] = 1.0 / (1e-3 + count)
+    column = jnp.broadcast_to(bias[...].astype(F32), (cols, bias.shape[1])).T
     for g in range(chans // 4):
         slab = [right[:, g * 4 + k].reshape(total, cols) for k in range(4)]
         rhs = jnp.concatenate(slab, axis=1)
@@ -87,7 +88,7 @@
     for h in range(rows // 2):
         lifted = jnp.dot(weight[...], outer_ref[h], preferred_element_type=F32)
         for k in range(2):
-            part = lifted[:, k * cols:(k + 1) * cols] + bias[...]
+            part = lifted[:, k * cols:(k + 1) * cols] + column
             part = part * scale_ref[h * 2 + k:h * 2 + k + 1, :]
             emit(h * 2 + k, part.T)
 
@@ -425,7 +426,7 @@
         vec = jnp.stack([ln_gamma, ln_beta, jnp.concatenate([b_a, b_b])], axis=1).astype(F32)
         both = project(msa.transpose(0, 2, 1), mask, vec, weight)
         lift = w_out.reshape(hidden, hidden, width).transpose(2, 1, 0).reshape(width, hidden * hidden)
-        bias_col = jnp.broadcast_to(b_out.astype(F32)[:, None], (width, J_STEP))
+        bias_col = b_out.reshape(1, width)
         tiled = pair.reshape(pair.shape[0], res // J_STEP, J_STEP, width)
         early, right, left = exchange(both, lift, bias_col, tiled)
         return finish(left, right, lift, bias_col, tiled, early)

time: 248 us -> 247 us (level)
  no operation moved by 1% of the time
where the time goes in v4:
time: 247 us; the launch traced here: 246 us
  Pallas kernels  240 us (97%)
  other arithmetic  2.75 us (1%)
  local copies, waits for them, and re-layouts  2.63 us (1%)
    pallas_call x1, Pallas kernels, exchange(): pl.pallas_call(exchange_kernel, in_specs=[hbm, vmem, vmem, hbm], out_spec...  178 us
    pallas_call x1, Pallas kernels, finish(): pl.pallas_call(finish_kernel, grid=(rest, rows // I_STEP), in_specs=[pl.B...  56.9 us
    pallas_call x1, Pallas kernels, project(): pl.pallas_call(project_kernel, grid=(seqs // S_STEP,), in_specs=[pl.Block...  5.52 us

profile of v4, /device:TPU:0, one launch (start us, length us, event | category | flops | bytes accessed | tf_op | source)
XLA Modules:
  0.0 245.7 jit_solution(2246714412074173551)
XLA Ops:
  0.0 0.7 maximum_bitcast_fusion
  0.7 0.7 maximum_convert_fusion
  1.4 1.3 pad_maximum_fusion.weight_ref
  2.8 0.7 copy.31.vec_ref
  3.5 1.1 copy.32
  4.5 0.9 copy.33.lift.weight_ref
  5.4 5.5 %project.1.both = bf16[2,4,33,32,128]{4,3,2,1,0:T(8,128)(2,1)} custom-call(bf16[32,64,512]{2,1,0:T(8,128)(2,1)} %bitcast.17, s32[32,512]{1,0:T(8,128)} %mask_ref.1, f32[64,3]{1,0:T(8,128)} %copy.31.vec_ref, bf16[64,64]{1,0:T(8,128)(2,1)} %pad_maximum_fusion.weight_ref), custom_call_target="tpu_custom_call" | custom-call | tf_op jit(solution)/shard_map/project/pallas_call | solution.py:46
  10.9 177.9 %exchange.1 = (f32[128,2,128,128]{3,2,1,0:T(8,128)}, bf16[2,16,33,32,128]{4,3,2,1,0:T(8,128)(2,1)}, bf16[4,4,1056,128]{3,2,1,0:T(8,128)(2,1)}) custom-call(bf16[2,4,33,32,128]{4,3,2,1,0:T(8,128)(2,1)} %project.1.both, bf16[128,1024]{1,0:T(8,128)(2,1)} %copy.33.lift.weight_ref, bf16[1,128]{1,0:T(2,128)(2,1)} %bitcast.22, f32[128,4,128,128]{3,2,1,0:T(8,128)} %bitcast.15), custom_call_target="tpu_custom_call" | custom-call | tf_op jit(solution)/shard_map/exchange/pallas_call | solution.py:356
  188.8 56.9 %finish.1 = f32[128,2,2,128,128]{4,3,2,1,0:T(8,128)} custom-call(bf16[4,4,1056,128]{3,2,1,0:T(8,128)(2,1)} %get-tuple-element.8.left_ref, bf16[2,16,33,32,128]{4,3,2,1,0:T(8,128)(2,1)} %get-tuple-element.9.right_ref, bf16[128,1024]{1,0:T(8,128)(2,1)} %copy.33.lift.weight_ref, bf16[1,128]{1,0:T(2,128)(2,1)} %bitcast.23, f32[128,2,2,128,128]{4,3,2,1,0:T(8,128)} %bitcast.16, ...), custom_call_target="tpu_custom_call" | custom-call | tf_op jit(solution)/shard_map/finish/pallas_call | solution.py:396
